TPU v7x, 32 devices: a whole 2x2x4 slice. The times are simulated.
32 devices in a mesh: cx: 4 (over z), cy: 2 (over y), tp: 4 (over x, core).
Axes of the slice: x: 2, y: 2, z: 4, core: 2. Of those that a mesh axis runs over, the one named last changes fastest.
Arguments:
- neighbor_ids: int32 [16, 8, 128], P(('cx', 'cy'), 'tp'), may hold values from 0 to 1023
- decoder: bfloat16 [16, 64, 896], P(('cx', 'cy')), may hold values from -6 to 6
- table: bfloat16 [1024, 896], P(('cx', 'cy')), may hold values from -6 to 6
- attn_in: bfloat16 [6, 896, 896], P(None, ('cx', 'cy'), 'tp'), may hold values from -0.1875 to 0.1875
- attn_out: bfloat16 [2, 896, 896], P(None, 'tp', ('cx', 'cy')), may hold values from -0.1875 to 0.1875
- gains: float32 [3, 896], replicated, may hold values from 0.25 to 1.75
- w_up: bfloat16 [896, 3584], P(('cx', 'cy'), 'tp'), may hold values from -0.1875 to 0.1875
- w_down: bfloat16 [3584, 896], P('tp', ('cx', 'cy')), may hold values from -0.09375 to 0.09375
Outputs:
- encoded: bfloat16 [16, 8, 128, 896], P(('cx', 'cy'), 'tp')
All inputs are finite; a program needn't handle non-finite values.
Results may differ from a plain program's by a relative error of at most 0.013.
Values may be sent and summed in bfloat16 or wider, within the bound.
No kernel may reach another device: no remote copies, remote signals or barrier semaphores. Data moves between devices by JAX's collectives and lax.ppermute only.
A program may use at most 128 MiB of HBM per device.

v0:
```python
import jax
import jax.numpy as jnp
from jax import lax
from jax.sharding import PartitionSpec as P

HD = 64


def layer_norm(values, gain):
    middle = jnp.mean(values, axis=-1, keepdims=True)
    centred = values - middle
    spread = jnp.mean(centred * centred, axis=-1, keepdims=True)
    return (centred * lax.rsqrt(spread + 1e-05) * gain).astype(jnp.bfloat16)


def project(hidden, matrix):
    return jnp.dot(hidden, matrix, preferred_element_type=jnp.float32).astype(jnp.bfloat16)


def attend(query, key_rows, value_rows):
    batch, q_len, width = query.shape
    k_len = key_rows.shape[1]
    heads = width // HD
    q_heads = query.reshape(batch, q_len, heads, HD)
    k_heads = key_rows.reshape(batch, k_len, heads, HD)
    v_heads = value_rows.reshape(batch, k_len, heads, HD)
    scores = jnp.einsum(
        "bqhd,bkhd->bhqk", q_heads, k_heads, preferred_element_type=jnp.float32
    ) * HD ** (-0.5)
    probs = jax.nn.softmax(scores, axis=-1).astype(jnp.bfloat16)
    mixed = jnp.einsum("bhqk,bkhd->bqhd", probs, v_heads, preferred_element_type=jnp.float32)
    return mixed.reshape(batch, q_len, width).astype(jnp.bfloat16)


def body(neighbor_ids, decoder, table, attn_in, attn_out, gains, w_up, w_down):
    full_table, in_w, out_w, up_w, down_w = (
        lax.all_gather(table, ("cx", "cy"), axis=0, tiled=True),
        lax.all_gather(attn_in, ("cx", "cy"), axis=1, tiled=True),
        lax.all_gather(attn_out, ("cx", "cy"), axis=2, tiled=True),
        lax.all_gather(w_up, ("cx", "cy"), axis=0, tiled=True),
        lax.all_gather(w_down, ("cx", "cy"), axis=1, tiled=True),
    )
    spans, nbrs, length = neighbor_ids.shape
    width = full_table.shape[1]
    dec_len = decoder.shape[1]
    total = spans * nbrs * length
    dec_rows = decoder.reshape(spans * dec_len, width)
    x_zero = jnp.take(full_table, neighbor_ids.reshape(-1), axis=0).astype(jnp.float32)
    h_one = layer_norm(x_zero, gains[0])
    in_full, out_full = (
        lax.all_gather(in_w, "tp", axis=2, tiled=True),
        lax.all_gather(out_w, "tp", axis=1, tiled=True),
    )
    query = project(h_one, in_full[0]).reshape(spans * nbrs, length, width)
    keys = project(h_one, in_full[1]).reshape(spans * nbrs, length, width)
    values = project(h_one, in_full[2]).reshape(spans * nbrs, length, width)
    self_out = attend(query, keys, values).reshape(total, width)
    x_one = x_zero + jnp.dot(self_out, out_full[0], preferred_element_type=jnp.float32)
    h_two = layer_norm(x_one, gains[1])
    cross_q = project(h_two, in_full[3]).reshape(spans, nbrs * length, width)
    cross_k = project(dec_rows, in_full[4]).reshape(spans, dec_len, width)
    cross_v = project(dec_rows, in_full[5]).reshape(spans, dec_len, width)
    cross = attend(cross_q, cross_k, cross_v).reshape(total, width)
    x_two = x_one + jnp.dot(cross, out_full[1], preferred_element_type=jnp.float32)
    h_three = layer_norm(x_two, gains[2])
    every = lax.all_gather(h_three, "tp", axis=0, tiled=True)
    upward = jnp.dot(every, up_w, preferred_element_type=jnp.float32)
    act = jax.nn.gelu(upward, approximate=True).astype(jnp.bfloat16)
    mixed = lax.psum_scatter(
        jnp.dot(act, down_w, preferred_element_type=jnp.float32).astype(jnp.bfloat16),
        "tp",
        scatter_dimension=0,
        tiled=True,
    ).astype(jnp.float32)
    return (x_two + mixed).astype(jnp.bfloat16).reshape(spans, nbrs, length, width)


def solution(mesh):
    in_specs = (
        P(("cx", "cy"), "tp", None),
        P(("cx", "cy"), None, None),
        P(("cx", "cy"), None),
        P(None, ("cx", "cy"), "tp"),
        P(None, "tp", ("cx", "cy")),
        P(),
        P(("cx", "cy"), "tp"),
        P("tp", ("cx", "cy")),
    )
    out_specs = P(("cx", "cy"), "tp", None, None)
    return jax.shard_map(body, mesh=mesh, in_specs=in_specs, out_specs=out_specs, check_vma=False)
```

profile of v0, /device:TPU:0, one launch (start us, length us, event | category | flops | bytes accessed | tf_op | source)
XLA Modules:
  0.0 414.2 jit_solution(9565664598188071752)
XLA Ops:
  6.5 1.9 copy.66
  9.3 69.2 %all-gather.10.cloned.1.call-done = bf16[6,896,224]{2,0,1:T(8,128)(2,1)} async-done(((bf16[6,112,224]{2,0,1:T(8,128)(2,1)}), bf16[6,896,224]{2,0,1:T(8,128)(2,1)}) %all-gather.10.cloned.1.call-update) | async-done | bytes 2408464 | tf_op jit(solution)/shard_map/all_gather | solution.py:38
  78.5 6.1 %copy.67 = bf16[6,896,224]{1,2,0:T(8,128)(2,1)} copy(bf16[6,896,224]{2,0,1:T(8,128)(2,1)} %all-gather.10.cloned.1.call-done) | data formatting | bytes 4816896 | tf_op jit(solution)/shard_map/all_gather | solution.py:38
  85.6 34.5 %all_gather.27 = bf16[2,224,896]{1,0,2:T(2,128)(2,1)S(1)} all-gather(bf16[2,224,112]{1,0,2:T(2,128)(2,1)S(1)} %copy.76), channel_id=1, replica_groups=mesh['cx'=4,'cy'=2,'tp'=4] {'cx','cy'}, dimensions={2}, use_global_device_ids=true | all-gather | bytes 903168 | tf_op jit(solution)/shard_map/all_gather | solution.py:39
  120.1 2.2 copy.77
  123.7 7.4 %all-gather.8.cloned.1.call-done = bf16[1024,896]{1,0:T(8,128)(2,1)} async-done(((bf16[128,896]{1,0:T(8,128)(2,1)}), bf16[1024,896]{1,0:T(8,128)(2,1)}) %all-gather.8.cloned.1.call-update) | async-done | bytes 1835024 | tf_op jit(solution)/shard_map/all_gather | solution.py:37
  131.1 4.3 %gather_fusion = bf16[512,896]{1,0:T(8,128)(2,1)S(1)} fusion(bf16[1024,896]{1,0:T(8,128)(2,1)} %all-gather.8.cloned.1.call-done, s32[1024]{0:T(1024)S(1)} %pad_clamp_fusion), kind=kCustom, calls=%fused_computation | custom fusion | bytes 1837056 | tf_op jit(solution)/shard_map/jit(_take)/gather | solution.py:48
  136.2 61.5 %all-gather.12.cloned.1.call-done = bf16[6,896,896]{1,2,0:T(8,128)(2,1)} async-done(((bf16[6,896,224]{1,2,0:T(8,128)(2,1)}), bf16[6,896,896]{1,2,0:T(8,128)(2,1)}) %all-gather.12.cloned.1.call-update) | async-done | bytes 9633808 | tf_op jit(solution)/shard_map/all_gather | solution.py:51
  197.7 3.8 fusion.46
  201.5 2.9 reshape.106
  204.4 3.9 fusion.47
  208.3 4.0 reshape.107
  212.3 3.0 fusion.29
  215.3 2.7 fusion.82
  218.0 3.8 fusion.45
  221.7 3.1 reshape.105
  224.8 2.8 fusion.52
  228.4 2.8 fusion.83
  232.4 2.8 fusion.48
  235.1 1.4 reshape.109
  236.6 2.1 fusion.57
  239.0 2.7 fusion.56
  241.7 1.3 reshape.108
  243.8 1.2 copy-done.4
  245.5 2.2 fusion.55
  249.3 2.8 fusion.85
  253.7 21.0 %all-gather.18.cloned.1.call-done = bf16[896,896]{1,0:T(8,128)(2,1)} async-done(((bf16[112,896]{1,0:T(8,128)(2,1)}), bf16[896,896]{1,0:T(8,128)(2,1)}) %all-gather.18.cloned.1.call-update) | async-done | bytes 1605648 | tf_op jit(solution)/shard_map/all_gather | solution.py:40
  274.7 45.0 %all-gather.20.cloned.1.call-done = bf16[896,896]{0,1:T(8,128)(2,1)} async-done(((bf16[896,112]{0,1:T(8,128)(2,1)}), bf16[896,896]{0,1:T(8,128)(2,1)}) %all-gather.20.cloned.1.call-update) | async-done | bytes 1605648 | tf_op jit(solution)/shard_map/all_gather | solution.py:41
  319.7 31.4 %all-gather.16.cloned.1.call-done = bf16[2048,896]{1,0:T(8,128)(2,1)} async-done(((bf16[512,896]{1,0:T(8,128)(2,1)}), bf16[2048,896]{1,0:T(8,128)(2,1)}) %all-gather.16.cloned.1.call-update) | async-done | bytes 3670032 | tf_op jit(solution)/shard_map/all_gather | solution.py:66
  351.1 12.6 %fusion.16 = bf16[2048,896]{1,0:T(8,128)(2,1)} fusion(bf16[896,896]{0,1:T(8,128)(2,1)} %all-gather.20.cloned.1.call-done, bf16[2048,896]{1,0:T(8,128)(2,1)} %all-gather.16.cloned.1.call-done, bf16[896,896]{1,0:T(8,128)(2,1)} %all-gather.18.cloned.1.call-done), kind=kOutput, calls=%fused_computation.19 | convolution fusion | flops 6595018752 | bytes 10551296 | tf_op jit(solution)/shard_map/dot_general | solution.py:70
  363.7 41.4 %reduce-scatter.2.cloned.1.call-done = bf16[512,896]{1,0:T(8,128)(2,1)} async-done(((bf16[2048,896]{1,0:T(8,128)(2,1)}), bf16[512,896]{1,0:T(8,128)(2,1)}) %reduce-scatter.2.cloned.1.call-update) | async-done | bytes 917520 | tf_op jit(solution)/shard_map/reduce_scatter | solution.py:69
  405.1 2.3 add_convert_fusion
  (54 shorter events, 10.6 us)
Async XLA Ops:
  6.5 230.0 %copy-start = (bf16[2,64,896]{2,1,0:T(8,128)(2,1)S(1)}, bf16[2,64,896]{2,1,0:T(8,128)(2,1)}, u32[]{:S(2)}) copy-start(bf16[2,64,896]{2,1,0:T(8,128)(2,1)} %param.9) | copy-start | bytes 688132
  6.5 71.9 %all-gather.10.cloned.1.call-start = ((), (), s32[]{:S(2)}) async-start(), calls=%async_computation.2 | async-start | bytes 4128768 | tf_op jit(solution)/shard_map/all_gather | solution.py:38
  8.5 122.6 %all-gather.8.cloned.1.call-start = ((), (), s32[]{:S(2)}) async-start(), calls=%async_computation.1 | async-start | bytes 2064384 | tf_op jit(solution)/shard_map/all_gather | solution.py:37
  9.2 188.5 %all-gather.12.cloned.1.call-start = ((), (), s32[]{:S(2)}) async-start(), calls=%async_computation.3 | async-start | bytes 12042240 | tf_op jit(solution)/shard_map/all_gather | solution.py:51
  84.6 0.9 copy-start.5
  84.6 143.8 %all-gather.14.cloned.1.call-start = ((), (), s32[]{:S(2)}) async-start(), calls=%async_computation.4 | async-start | bytes 4014080 | tf_op jit(solution)/shard_map/all_gather | solution.py:52
  85.6 38.0 %copy-start.6 = (s32[2,2,128]{2,1,0:T(2,128)S(1)}, s32[2,2,128]{2,1,0:T(2,128)}, u32[]{:S(2)}) copy-start(s32[2,2,128]{2,1,0:T(2,128)} %param.8) | copy-start | bytes 6148
  85.6 38.0 %copy-start.7 = (f32[3,896]{1,0:T(4,128)S(1)}, f32[3,896]{1,0:T(4,128)}, u32[]{:S(2)}) copy-start(f32[3,896]{1,0:T(4,128)} %param.13) | copy-start | bytes 32260
  122.4 152.3 %all-gather.18.cloned.1.call-start = ((), (), s32[]{:S(2)}) async-start(), calls=%async_computation.6 | async-start | bytes 1806336 | tf_op jit(solution)/shard_map/all_gather | solution.py:40
  122.9 196.7 %all-gather.20.cloned.1.call-start = ((), (), s32[]{:S(2)}) async-start(), calls=%async_computation.7 | async-start | bytes 1806336 | tf_op jit(solution)/shard_map/all_gather | solution.py:41
  123.5 227.6 %all-gather.16.cloned.1.call-start = ((), (), s32[]{:S(2)}) async-start(), calls=%async_computation.5 | async-start | bytes 4587520 | tf_op jit(solution)/shard_map/all_gather | solution.py:66
  231.2 1.2 copy-start.2
  243.8 1.3 copy-start.4
  247.8 1.5 copy-start.3
  253.7 151.4 %reduce-scatter.2.cloned.1.call-start = ((), (), s32[]{:S(2)}) async-start(), calls=%async_computation.8 | async-start | bytes 4587520 | tf_op jit(solution)/shard_map/reduce_scatter | solution.py:69
  363.7 43.6 %copy-start.1 = (bf16[2,64,896]{2,1,0:T(8,128)(2,1)S(1)}, bf16[2,64,896]{2,1,0:T(8,128)(2,1)}, u32[]{:S(2)}) copy-start(bf16[2,64,896]{2,1,0:T(8,128)(2,1)} %param.9) | copy-start | bytes 688132
Sparse Core Ops, SparseCore 0:
  9.5 68.9 all-gather.9
  80.7 50.3 all-gather.7
  132.6 65.0 all-gather.11
  199.1 28.8 all-gather.13
  230.1 44.5 all-gather.17
  276.7 42.9 all-gather.19
  321.2 29.8 all-gather.15
  363.8 41.2 reduce-scatter.1
where the time goes:
time: 415 us; the launch traced here: 414 us
  waiting for transfers between devices  279 us (67%)
  matrix products  45.8 us (11%)
  blocking collectives  34.5 us (8%)
  local copies, waits for them, and re-layouts  32.9 us (8%)
  between operations  13.7 us (3%)
  other arithmetic  8.18 us (2%)
    all_gather x1, waiting for transfers between devices, body(): lax.all_gather(attn_in, ('cx', 'cy'), axis=1, tiled=True)  69.2 us
    all_gather x1, waiting for transfers between devices, body(): lax.all_gather(in_w, 'tp', axis=2, tiled=True)  61.5 us
    all_gather x1, waiting for transfers between devices, body(): lax.all_gather(w_down, ('cx', 'cy'), axis=1, tiled=True)  45 us
    reduce_scatter x1, waiting for transfers between devices, body(): lax.psum_scatter(jnp.dot(act, down_w, preferred_element_type=jnp.float32)...  41.4 us
    all_gather x1, blocking collectives, body(): lax.all_gather(attn_out, ('cx', 'cy'), axis=2, tiled=True)  34.5 us
    all_gather x1, waiting for transfers between devices, body(): every = lax.all_gather(h_three, 'tp', axis=0, tiled=True)  31.4 us
    all_gather x1, waiting for transfers between devices, body(): lax.all_gather(w_up, ('cx', 'cy'), axis=0, tiled=True)  21 us
    dot_general x6, matrix products, project(): jnp.dot(hidden, matrix, preferred_element_type=jnp.float32)  18.9 us
  transfers between devices with their start and end apart: 8, of which 7 were waited for; matrix products, arithmetic and copies ran while one was open for 16% of the time, Pallas kernels for 0%

commit v1 on v0

--- a/solution.py
+++ b/solution.py
@@ -63,7 +63,9 @@
     cross = attend(cross_q, cross_k, cross_v).reshape(total, width)
     x_two = x_one + jnp.dot(cross, out_full[1], preferred_element_type=jnp.float32)
     h_three = layer_norm(x_two, gains[2])
-    every = lax.all_gather(h_three, "tp", axis=0, tiled=True)
+    every = jnp.concatenate(
+        lax.all_to_all(jnp.stack([h_three] * lax.axis_size("tp")), "tp", 0, 0), axis=0
+    )
     upward = jnp.dot(every, up_w, preferred_element_type=jnp.float32)
     act = jax.nn.gelu(upward, approximate=True).astype(jnp.bfloat16)
     mixed = lax.psum_scatter(

time: 415 us -> 382 us (0.920)
  waiting for transfers between devices: 279 us -> 241 us
  starting transfers between devices: 0.28 us -> 5.04 us
    all_gather x1 -> x0, waiting for transfers between devices: 31.4 us -> none  [body(): every = lax.all_gather(h_three, 'tp', axis=0, tiled=True)]
    all_to_all x0 -> x1, starting transfers between devices: none -> 4.8 us  [body(): lax.all_to_all(jnp.stack([h_three] * lax.axis_size('tp')), 'tp', 0, 0)]
    all_gather x1, waiting for transfers between devices: 21 us -> 16.6 us  [body(): lax.all_gather(w_up, ('cx', 'cy'), axis=0, tiled=True)]
  transfers between devices with their start and end apart: 8 -> 8, of which waited for: 7 -> 6; matrix products, arithmetic and copies ran while one was open for 16% -> 17% of each run, Pallas kernels for 0% -> 0%
where the time goes in v1:
time: 382 us; the launch traced here: 381 us
  waiting for transfers between devices  241 us (63%)
  matrix products  45.1 us (12%)
  blocking collectives  34.5 us (9%)
  local copies, waits for them, and re-layouts  34.1 us (9%)
  between operations  13.8 us (4%)
  other arithmetic  7.26 us (2%)
  starting transfers between devices  5.04 us (1%)
    all_gather x1, waiting for transfers between devices, body(): lax.all_gather(attn_in, ('cx', 'cy'), axis=1, tiled=True)  69.2 us
    all_gather x1, waiting for transfers between devices, body(): lax.all_gather(in_w, 'tp', axis=2, tiled=True)  61.5 us
    all_gather x1, waiting for transfers between devices, body(): lax.all_gather(w_down, ('cx', 'cy'), axis=1, tiled=True)  44.9 us
    reduce_scatter x1, waiting for transfers between devices, body(): lax.psum_scatter(jnp.dot(act, down_w, preferred_element_type=jnp.float32)...  39.7 us
    all_gather x1, blocking collectives, body(): lax.all_gather(attn_out, ('cx', 'cy'), axis=2, tiled=True)  34.5 us
    dot_general x6, matrix products, project(): jnp.dot(hidden, matrix, preferred_element_type=jnp.float32)  18.2 us
    all_gather x1, waiting for transfers between devices, body(): lax.all_gather(w_up, ('cx', 'cy'), axis=0, tiled=True)  16.6 us
    dot_general x1, matrix products, body(): jnp.dot(act, down_w, preferred_element_type=jnp.float32)  12.6 us
  transfers between devices with their start and end apart: 8, of which 6 were waited for; matrix products, arithmetic and copies ran while one was open for 17% of the time, Pallas kernels for 0%

profile of v1, /device:TPU:0, one launch (start us, length us, event | category | flops | bytes accessed | tf_op | source)
XLA Modules:
  0.0 381.0 jit_solution(6120966384473412586)
XLA Ops:
  6.5 1.9 copy.66
  9.3 69.2 %all-gather.9.cloned.1.call-done = bf16[6,896,224]{2,0,1:T(8,128)(2,1)} async-done(((bf16[6,112,224]{2,0,1:T(8,128)(2,1)}), bf16[6,896,224]{2,0,1:T(8,128)(2,1)}) %all-gather.9.cloned.1.call-update) | async-done | bytes 2408464 | tf_op jit(solution)/shard_map/all_gather | solution.py:38
  78.5 6.1 %copy.67 = bf16[6,896,224]{1,2,0:T(8,128)(2,1)} copy(bf16[6,896,224]{2,0,1:T(8,128)(2,1)} %all-gather.9.cloned.1.call-done) | data formatting | bytes 4816896 | tf_op jit(solution)/shard_map/all_gather | solution.py:38
  85.6 34.5 %all_gather.24 = bf16[2,224,896]{1,0,2:T(2,128)(2,1)S(1)} all-gather(bf16[2,224,112]{1,0,2:T(2,128)(2,1)S(1)} %copy.76), channel_id=1, replica_groups=mesh['cx'=4,'cy'=2,'tp'=4] {'cx','cy'}, dimensions={2}, use_global_device_ids=true | all-gather | bytes 903168 | tf_op jit(solution)/shard_map/all_gather | solution.py:39
  120.1 2.2 copy.77
  123.6 7.5 %all-gather.7.cloned.1.call-done = bf16[1024,896]{1,0:T(8,128)(2,1)} async-done(((bf16[128,896]{1,0:T(8,128)(2,1)}), bf16[1024,896]{1,0:T(8,128)(2,1)}) %all-gather.7.cloned.1.call-update) | async-done | bytes 1835024 | tf_op jit(solution)/shard_map/all_gather | solution.py:37
  131.1 4.3 %gather_fusion = bf16[512,896]{1,0:T(8,128)(2,1)S(1)} fusion(bf16[1024,896]{1,0:T(8,128)(2,1)} %all-gather.7.cloned.1.call-done, s32[1024]{0:T(1024)S(1)} %pad_clamp_fusion), kind=kCustom, calls=%fused_computation | custom fusion | bytes 1837056 | tf_op jit(solution)/shard_map/jit(_take)/gather | solution.py:48
  136.2 61.5 %all-gather.11.cloned.1.call-done = bf16[6,896,896]{1,2,0:T(8,128)(2,1)} async-done(((bf16[6,896,224]{1,2,0:T(8,128)(2,1)}), bf16[6,896,896]{1,2,0:T(8,128)(2,1)}) %all-gather.11.cloned.1.call-update) | async-done | bytes 9633808 | tf_op jit(solution)/shard_map/all_gather | solution.py:51
  197.7 3.8 fusion.46
  201.5 2.9 reshape.112
  204.4 3.9 %fusion.47 = bf16[512,896]{1,0:T(8,128)(2,1)} fusion(bf16[6,896,896]{1,2,0:T(8,128)(2,1)} %all-gather.11.cloned.1.call-done, f32[896]{0:T(1024)S(1)} %get-tuple-element.6, f32[512]{0:T(512)S(1)} %add_rsqrt_fusion.2, f32[512]{0:T(512)S(1)} %broadcast_multiply_fusion.2, bf16[512,896]{1,0:T(8,128)(2,1)S(1)} %gather_fusion, pred[512]{0:T(512)(128)(4,1)S(1)} %compare_and_fusion), kind=kOutput, calls=%fused_computation.66 | convolution fusion | flops 825294848 | bytes 3448832 | tf_op jit(solution)/shard_map/dot_general | solution.py:17
  208.3 4.0 %reshape.113 = bf16[4,128,14,64]{3,2,1,0:T(8,128)(2,1)} reshape(bf16[512,896]{1,0:T(8,128)(2,1)} %fusion.47) | data formatting | bytes 1835008 | tf_op jit(solution)/shard_map/reshape;reshape | solution.py:25
  212.3 3.0 fusion.29
  215.3 2.7 fusion.82
  218.0 3.8 fusion.45
  221.7 3.1 reshape.111
  224.8 2.8 fusion.52
  228.4 2.8 fusion.83
  232.4 2.8 fusion.48
  235.1 1.4 reshape.115
  236.6 2.1 fusion.57
  239.8 1.2 copy-done.4
  241.5 2.0 fusion.56
  243.9 2.2 fusion.55
  247.7 2.8 fusion.85
  251.1 2.1 stack.2
  253.3 4.8 %all-to-all-start = ((bf16[4,512,896]{2,1,0:T(8,128)(2,1)}), bf16[4,512,896]{2,1,0:T(8,128)(2,1)}, u32[]{:S(2)}, u32[]{:S(2)}) async-start(bf16[4,512,896]{2,1,0:T(8,128)(2,1)} %stack.2), calls=%async_computation | async-start | bytes 7340032 | tf_op jit(solution)/shard_map/all_to_all | solution.py:67
  258.1 16.6 %all-gather.15.cloned.1.call-done = bf16[896,896]{1,0:T(8,128)(2,1)} async-done(((bf16[112,896]{1,0:T(8,128)(2,1)}), bf16[896,896]{1,0:T(8,128)(2,1)}) %all-gather.15.cloned.1.call-update) | async-done | bytes 1605648 | tf_op jit(solution)/shard_map/all_gather | solution.py:40
  274.7 44.9 %all-gather.17.cloned.1.call-done = bf16[896,896]{0,1:T(8,128)(2,1)} async-done(((bf16[896,112]{0,1:T(8,128)(2,1)}), bf16[896,896]{0,1:T(8,128)(2,1)}) %all-gather.17.cloned.1.call-update) | async-done | bytes 1605648 | tf_op jit(solution)/shard_map/all_gather | solution.py:41
  319.6 12.6 %fusion.16 = bf16[2048,896]{1,0:T(8,128)(2,1)} fusion(bf16[896,896]{0,1:T(8,128)(2,1)} %all-gather.17.cloned.1.call-done, bf16[2048,896]{1,0:T(8,128)(2,1)} %bitcast.14, bf16[896,896]{1,0:T(8,128)(2,1)} %all-gather.15.cloned.1.call-done), kind=kOutput, calls=%fused_computation.19 | convolution fusion | flops 6595018752 | bytes 10551296 | tf_op jit(solution)/shard_map/dot_general | solution.py:72
  332.2 39.7 %reduce-scatter.2.cloned.1.call-done = bf16[512,896]{1,0:T(8,128)(2,1)} async-done(((bf16[2048,896]{1,0:T(8,128)(2,1)}), bf16[512,896]{1,0:T(8,128)(2,1)}) %reduce-scatter.2.cloned.1.call-update) | async-done | bytes 917520 | tf_op jit(solution)/shard_map/reduce_scatter | solution.py:71
  371.9 2.3 add_convert_fusion
  (54 shorter events, 10.0 us)
Async XLA Ops:
  6.5 230.0 %copy-start = (bf16[2,64,896]{2,1,0:T(8,128)(2,1)S(1)}, bf16[2,64,896]{2,1,0:T(8,128)(2,1)}, u32[]{:S(2)}) copy-start(bf16[2,64,896]{2,1,0:T(8,128)(2,1)} %param.9) | copy-start | bytes 688132
  6.5 71.9 %all-gather.9.cloned.1.call-start = ((), (), s32[]{:S(2)}) async-start(), calls=%async_computation.3 | async-start | bytes 4128768 | tf_op jit(solution)/shard_map/all_gather | solution.py:38
  8.5 122.6 %all-gather.7.cloned.1.call-start = ((), (), s32[]{:S(2)}) async-start(), calls=%async_computation.2 | async-start | bytes 2064384 | tf_op jit(solution)/shard_map/all_gather | solution.py:37
  9.2 188.5 %all-gather.11.cloned.1.call-start = ((), (), s32[]{:S(2)}) async-start(), calls=%async_computation.4 | async-start | bytes 12042240 | tf_op jit(solution)/shard_map/all_gather | solution.py:51
  84.6 0.9 copy-start.5
  84.6 143.8 %all-gather.13.cloned.1.call-start = ((), (), s32[]{:S(2)}) async-start(), calls=%async_computation.5 | async-start | bytes 4014080 | tf_op jit(solution)/shard_map/all_gather | solution.py:52
  85.6 37.9 %copy-start.6 = (s32[2,2,128]{2,1,0:T(2,128)S(1)}, s32[2,2,128]{2,1,0:T(2,128)}, u32[]{:S(2)}) copy-start(s32[2,2,128]{2,1,0:T(2,128)} %param.8) | copy-start | bytes 6148
  85.6 38.0 %copy-start.7 = (f32[3,896]{1,0:T(4,128)S(1)}, f32[3,896]{1,0:T(4,128)}, u32[]{:S(2)}) copy-start(f32[3,896]{1,0:T(4,128)} %param.13) | copy-start | bytes 32260
  122.4 152.3 %all-gather.15.cloned.1.call-start = ((), (), s32[]{:S(2)}) async-start(), calls=%async_computation.6 | async-start | bytes 1806336 | tf_op jit(solution)/shard_map/all_gather | solution.py:40
  122.9 196.6 %all-gather.17.cloned.1.call-start = ((), (), s32[]{:S(2)}) async-start(), calls=%async_computation.7 | async-start | bytes 1806336 | tf_op jit(solution)/shard_map/all_gather | solution.py:41
  231.2 1.2 copy-start.2
  239.8 1.2 copy-start.4
  246.2 1.5 copy-start.3
  253.3 66.3 %all-to-all-start = ((bf16[4,512,896]{2,1,0:T(8,128)(2,1)}), bf16[4,512,896]{2,1,0:T(8,128)(2,1)}, u32[]{:S(2)}, u32[]{:S(2)}) async-start(bf16[4,512,896]{2,1,0:T(8,128)(2,1)} %stack.2), calls=%async_computation | async-start | bytes 7340032 | tf_op jit(solution)/shard_map/all_to_all | solution.py:67
  258.1 113.9 %reduce-scatter.2.cloned.1.call-start = ((), (), s32[]{:S(2)}) async-start(), calls=%async_computation.8 | async-start | bytes 4587520 | tf_op jit(solution)/shard_map/reduce_scatter | solution.py:71
  332.2 42.0 %copy-start.1 = (bf16[2,64,896]{2,1,0:T(8,128)(2,1)S(1)}, bf16[2,64,896]{2,1,0:T(8,128)(2,1)}, u32[]{:S(2)}) copy-start(bf16[2,64,896]{2,1,0:T(8,128)(2,1)} %param.9) | copy-start | bytes 688132
Sparse Core Ops, SparseCore 0:
  9.5 68.9 all-gather.8
  80.7 50.3 all-gather.6
  132.6 65.0 all-gather.10
  199.1 28.8 all-gather.12
  230.1 44.5 all-gather.14
  276.7 42.8 all-gather.16
  332.3 39.5 reduce-scatter.1
